TPU v7x, 32 devices: a whole 2x2x4 slice. The times are simulated.
32 devices in a mesh: occ: 8 (over z, y), aux: 4 (over x, core).
Axes of the slice: x: 2, y: 2, z: 4, core: 2. Of those that a mesh axis runs over, the one named last changes fastest.
Arguments:
- amplitudes: bfloat16 [2, 512, 2048], P(None, 'occ'), may hold values from -0.29882812 to 0.29882812
- fit_factor: bfloat16 [1024, 512, 2048], P('aux', 'occ'), may hold values from -0.14941406 to 0.14941406
Outputs:
- virtual_density: float32 [2, 2048, 2048], P(None, 'aux', 'occ')
- occupied_density: float32 [2, 512, 512], P(None, 'occ')
- right_side: float32 [2, 512, 2048], P(None, 'occ', 'aux')
All inputs are finite; a program needn't handle non-finite values.
Results may differ from a plain program's by a relative error of at most 0.0068.
Values may be sent and summed in bfloat16 or wider, within the bound.
A program may use at most 128 MiB of HBM per device.

v0:
```python
import jax
import jax.numpy as jnp
from jax import lax
from jax.experimental import pallas as pl
from jax.experimental.pallas import tpu as pltpu
from jax.sharding import PartitionSpec as P

SCATTER = True
NT = (((1,), (1,)), ((), ()))


def block_of(total, want):
    while total % want:
        want //= 2
    return want


def fit_kernel(x_ref, b_ref, out_ref):
    states, occ, virt = x_ref.shape
    count = b_ref.shape[0]
    wide = x_ref[...].reshape(states * occ, virt)
    pairs = lax.dot_general(
        b_ref[...].reshape(count * occ, virt), wide, NT, preferred_element_type=jnp.float32
    ).reshape(count, occ, states * occ)
    row = lax.broadcasted_iota(jnp.int32, pairs.shape, 1)
    col = lax.broadcasted_iota(jnp.int32, pairs.shape, 2)
    out_ref[...] = jnp.sum(jnp.where(col % occ == row, pairs, 0.0), axis=1)


def fit_part(amplitudes, factor):
    states, occ, virt = amplitudes.shape
    aux = factor.shape[0]
    count = block_of(aux, 16)
    sums = pl.pallas_call(
        fit_kernel,
        grid=(aux // count,),
        in_specs=[
            pl.BlockSpec((states, occ, virt), lambda k: (0, 0, 0)),
            pl.BlockSpec((count, occ, virt), lambda k: (k, 0, 0)),
        ],
        out_specs=pl.BlockSpec((count, states * occ), lambda k: (k, 0)),
        out_shape=jax.ShapeDtypeStruct((aux, states * occ), jnp.float32),
        compiler_params=pltpu.CompilerParams(vmem_limit_bytes=48 << 20),
        cost_estimate=pl.CostEstimate(
            flops=2 * states * aux * occ * occ * virt,
            bytes_accessed=2 * aux * occ * virt,
            transcendentals=0,
        ),
    )(amplitudes, factor)
    return jnp.sum(sums.reshape(aux, states, occ), axis=2).T


def field_kernel(f_ref, b_ref, out_ref):
    count, occ, virt = b_ref.shape
    states, depth = f_ref.shape
    spread = f_ref[...].astype(jnp.float32)
    row = lax.broadcasted_iota(jnp.int32, (occ, depth), 0)
    col = lax.broadcasted_iota(jnp.int32, (occ, depth), 1)
    keep = col % occ == row
    left = jnp.concatenate(
        [
            jnp.where(keep, jnp.broadcast_to(spread[s : s + 1], (occ, depth)), 0.0)
            for s in range(states)
        ],
        axis=0,
    ).astype(jnp.bfloat16)
    term = jnp.dot(
        left, b_ref[...].reshape(depth, virt), preferred_element_type=jnp.float32
    ).reshape(states, occ, virt)

    @pl.when(pl.program_id(0) == 0)
    def _():
        out_ref[...] = term

    @pl.when(pl.program_id(0) > 0)
    def _():
        out_ref[...] += term


def field_part(fitted, factor):
    states = fitted.shape[0]
    aux, occ, virt = factor.shape
    count = block_of(aux, 16)
    return pl.pallas_call(
        field_kernel,
        grid=(aux // count,),
        in_specs=[
            pl.BlockSpec((states, count * occ), lambda k: (0, k)),
            pl.BlockSpec((count, occ, virt), lambda k: (k, 0, 0)),
        ],
        out_specs=pl.BlockSpec((states, occ, virt), lambda k: (0, 0, 0)),
        out_shape=jax.ShapeDtypeStruct((states, occ, virt), jnp.float32),
        compiler_params=pltpu.CompilerParams(vmem_limit_bytes=48 << 20),
        cost_estimate=pl.CostEstimate(
            flops=2 * states * aux * occ * occ * virt,
            bytes_accessed=2 * aux * occ * virt,
            transcendentals=0,
        ),
    )(jnp.repeat(fitted, occ, axis=1), factor)


def body(amplitudes, fit_factor):
    high = lax.Precision.HIGHEST
    slab = lax.axis_index("aux")
    width = amplitudes.shape[2] // lax.axis_size("aux")
    own_cols = lax.dynamic_slice_in_dim(amplitudes, slab * width, width, 2)
    gathered = lax.all_gather(own_cols, "occ", axis=1, tiled=True)
    blocked = lax.all_to_all(amplitudes, "occ", split_axis=2, concat_axis=1, tiled=True)
    virtual_density = jnp.einsum(
        "sia,sib->sab", gathered, blocked, preferred_element_type=jnp.float32
    )
    pair_part = jnp.einsum("sia,sja->sij", own_cols, gathered, preferred_element_type=jnp.float32)
    occupied_density = lax.psum(pair_part, "aux")
    fitted = lax.psum(fit_part(amplitudes, fit_factor), "occ").astype(jnp.bfloat16)
    part = field_part(fitted, fit_factor)
    if SCATTER:
        field_cols = lax.psum_scatter(part, "aux", scatter_dimension=2, tiled=True).astype(jnp.bfloat16)
    else:
        field = lax.psum(part, "aux").astype(jnp.bfloat16)
        field_cols = lax.dynamic_slice_in_dim(field, slab * width, width, 2)
    second = jnp.einsum(
        "sij,sja->sia",
        occupied_density,
        lax.all_gather(field_cols, "occ", axis=1, tiled=True).astype(jnp.float32),
        precision=high,
    )
    cross_part = jnp.einsum(
        "sib,sjb->sij", field_cols, gathered, preferred_element_type=jnp.float32
    )
    cross = lax.psum(cross_part, "aux")
    first = jnp.einsum("sij,sja->sia", cross, gathered.astype(jnp.float32), precision=high)
    return (virtual_density, occupied_density, first - second)


def solution(mesh):
    placed = (P(None, "occ", None), P("aux", "occ", None))
    return jax.shard_map(
        body,
        mesh=mesh,
        in_specs=placed,
        out_specs=(P(None, "aux", "occ"), P(None, "occ", None), P(None, "occ", "aux")),
        check_vma=False,
    )
```

profile of v0, /device:TPU:0, one launch (start us, length us, event | category | flops | bytes accessed | tf_op | source)
XLA Modules:
  0.0 175.8 jit_solution(3254410505311884800)
XLA Ops:
  8.0 0.0 all-gather.3.cloned.1.call-start
  8.0 1.6 constant_dynamic-slice_fusion
  9.6 0.0 all-gather.3.cloned.1.call-update
  9.6 0.0 reduce-scatter.2.cloned.1.call-start
  9.7 1.0 copy-done
  10.7 30.3 %shard_map.49 = f32[256,128]{1,0:T(8,128)S(1)} custom-call(bf16[2,64,2048]{2,1,0:T(8,128)(2,1)S(1)} %copy-done, bf16[256,64,2048]{2,1,0:T(8,128)(2,1)} %b_ref.3), custom_call_target="tpu_custom_call" | custom-call | flops 8589934592 | bytes 67108864 | tf_op jit(solution)/shard_map/pallas_call | solution.py:34
  41.0 0.1 copy.10
  41.2 23.1 %psum.22 = bf16[2,256]{1,0:T(2,128)(2,1)S(1)} all-reduce(f32[2,256]{1,0:T(2,128)S(1)} %bitcast.22), channel_id=1, replica_groups=mesh['occ'=8,'aux'=4] {'occ'}, use_global_device_ids=true, to_apply=%region_2.0 | all-reduce | flops 512 | bytes 3072 | tf_op jit(solution)/shard_map/psum | solution.py:114
  64.3 0.1 broadcast_in_dim.3
  64.4 0.2 reshape.13.f_ref
  64.6 27.9 %shard_map.50 = f32[2,64,2048]{2,1,0:T(8,128)} custom-call(bf16[2,16384]{1,0:T(2,128)(2,1)S(1)} %reshape.13.f_ref, bf16[256,64,2048]{2,1,0:T(8,128)(2,1)} %b_ref.3), custom_call_target="tpu_custom_call" | custom-call | flops 8589934592 | bytes 67108864 | tf_op jit(solution)/shard_map/pallas_call | solution.py:84
  92.5 0.0 reduce-scatter.2.cloned.1.call-update
  92.5 0.0 all-reduce.3.cloned.1.call-start
  92.6 0.0 all-gather.3.cloned.1.call-done
  92.6 2.4 %fusion.1 = f32[2,64,512]{2,1,0:T(8,128)} fusion(bf16[2,64,512]{2,1,0:T(8,128)(2,1)S(1)} %copy-done.3, bf16[2,512,512]{2,1,0:T(8,128)(2,1)} %all-gather.3.cloned.1.call-done), kind=kOutput, calls=%fused_computation.4 | convolution fusion | flops 67108864 | bytes 1441792 | tf_op jit(solution)/shard_map/sia,sja->sij/dot_general | solution.py:112
  95.0 19.7 %reduce-scatter.2.cloned.1.call-done = f32[2,64,512]{2,1,0:T(8,128)} async-done(((f32[2,64,2048]{2,1,0:T(8,128)}), f32[2,64,512]{2,1,0:T(8,128)}) %reduce-scatter.2.cloned.1.call-update) | async-done | bytes 262160 | tf_op jit(solution)/shard_map/reduce_scatter | solution.py:117
  114.7 1.0 convert_element_type.9
  115.6 2.4 %fusion.2 = f32[2,64,512]{2,1,0:T(8,128)} fusion(bf16[2,64,512]{2,1,0:T(8,128)(2,1)S(1)} %convert_element_type.9, bf16[2,512,512]{2,1,0:T(8,128)(2,1)} %all-gather.3.cloned.1.call-done), kind=kOutput, calls=%fused_computation.5 | convolution fusion | flops 67108864 | bytes 1441792 | tf_op jit(solution)/shard_map/sib,sjb->sij/dot_general | solution.py:127
  118.1 0.0 all-reduce.3.cloned.1.call-update
  118.1 0.0 all-gather.5.cloned.1.call-start
  118.1 0.7 all-gather.5.cloned.1.call-update
  118.8 0.8 copy.8
  119.6 0.7 reshape.14
  120.3 23.8 %all_to_all.18 = bf16[8,2,16384]{2,1,0:T(2,128)(2,1)S(1)} all-to-all(bf16[8,2,16384]{2,1,0:T(2,128)(2,1)S(1)} %reshape.14), channel_id=1, replica_groups=mesh['occ'=8,'aux'=4] {'occ'}, dimensions={0} | all-to-all | bytes 1048576 | tf_op jit(solution)/shard_map/all_to_all | solution.py:108
  144.1 0.7 reshape.15
  144.8 0.7 copy.9
  145.5 2.7 %fusion = f32[2,512,256]{2,1,0:T(8,128)} fusion(bf16[2,512,512]{2,1,0:T(8,128)(2,1)} %all-gather.3.cloned.1.call-done, bf16[2,512,256]{2,1,0:T(8,128)(2,1)S(1)} %bitcast.21), kind=kOutput, calls=%fused_computation.3 | convolution fusion | flops 268435456 | bytes 2621440 | tf_op jit(solution)/shard_map/sia,sib->sab/dot_general | solution.py:109
  148.2 3.4 %all-reduce.3.cloned.1.call-done = (f32[2,64,512]{2,1,0:T(8,128)}, f32[2,64,512]{2,1,0:T(8,128)}) async-done(((f32[2,64,512]{2,1,0:T(8,128)}, f32[2,64,512]{2,1,0:T(8,128)}), (f32[2,64,512]{2,1,0:T(8,128)}, f32[2,64,512]{2,1,0:T(8,128)})) %all-reduce.3.cloned.1.call-update) | async-done | bytes 524304 | tf_op jit(solution)/shard_map/psum | solution.py:113
  151.6 2.0 %fusion.3 = f32[2,64,512]{2,1,0:T(8,128)S(1)} fusion(f32[2,64,512]{2,1,0:T(8,128)} %get-tuple-element.4, bf16[2,512,512]{2,1,0:T(8,128)(2,1)} %all-gather.3.cloned.1.call-done), kind=kOutput, calls=%fused_computation.6 | convolution fusion | flops 402653184 | bytes 1572864 | tf_op jit(solution)/shard_map/sij,sja->sia/dot_general | solution.py:131
  153.6 10.5 %all-gather.5.cloned.1.call-done = bf16[2,512,512]{2,1,0:T(8,128)(2,1)} async-done(((bf16[2,64,512]{2,1,0:T(8,128)(2,1)}), bf16[2,512,512]{2,1,0:T(8,128)(2,1)}) %all-gather.5.cloned.1.call-update) | async-done | bytes 1048592 | tf_op jit(solution)/shard_map/all_gather | solution.py:124
  164.1 2.7 %convolution_subtract_fusion = f32[2,64,512]{2,1,0:T(8,128)} fusion(f32[2,64,512]{2,1,0:T(8,128)S(1)} %fusion.3, f32[2,64,512]{2,1,0:T(8,128)} %get-tuple-element.6, bf16[2,512,512]{2,1,0:T(8,128)(2,1)} %all-gather.5.cloned.1.call-done), kind=kOutput, calls=%fused_computation | convolution fusion | flops 402718720 | bytes 1835008 | tf_op jit(solution)/shard_map/sij,sja->sia/dot_general | solution.py:121
  166.7 1.7 copy.13
  (8 shorter events, 0.0 us)
Async XLA Ops:
  8.0 84.6 %all-gather.3.cloned.1.call-start = ((), (), s32[]{:S(2)}) async-start(), calls=%async_computation.2 | async-start | bytes 1179648 | tf_op jit(solution)/shard_map/all_gather | solution.py:107
  9.6 105.0 %reduce-scatter.2.cloned.1.call-start = ((), (), s32[]{:S(2)}) async-start(), calls=%async_computation.3 | async-start | bytes 1310720 | tf_op jit(solution)/shard_map/reduce_scatter | solution.py:117
  9.7 1.0 copy-start
  10.7 81.9 %copy-start.3 = (bf16[2,64,512]{2,1,0:T(8,128)(2,1)S(1)}, bf16[2,64,512]{2,1,0:T(8,128)(2,1)}, u32[]{:S(2)}) copy-start(bf16[2,64,512]{2,1,0:T(8,128)(2,1)} %constant_dynamic-slice_fusion) | copy-start | bytes 393220
  10.7 108.1 %copy-start.1 = (bf16[2,64,2048]{2,1,0:T(8,128)(2,1)S(1)}, bf16[2,64,2048]{2,1,0:T(8,128)(2,1)}, u32[]{:S(2)}) copy-start(bf16[2,64,2048]{2,1,0:T(8,128)(2,1)} %x_ref.1) | copy-start | bytes 1572868
  92.5 59.1 %all-reduce.3.cloned.1.call-start = ((), (), s32[]{:S(2)}) async-start(), calls=%async_computation.5 | async-start | bytes 1048576 | tf_op jit(solution)/shard_map/psum | solution.py:113
  115.6 2.5 %copy-start.2 = (bf16[2,64,512]{2,1,0:T(8,128)(2,1)}, bf16[2,64,512]{2,1,0:T(8,128)(2,1)S(1)}, u32[]{:S(2)}) copy-start(bf16[2,64,512]{2,1,0:T(8,128)(2,1)S(1)} %convert_element_type.9) | copy-start | bytes 393220
  118.1 46.0 %all-gather.5.cloned.1.call-start = ((), (), s32[]{:S(2)}) async-start(), calls=%async_computation.4 | async-start | bytes 1179648 | tf_op jit(solution)/shard_map/all_gather | solution.py:124
Sparse Core Ops, SparseCore 0:
  11.6 42.9 all-gather.2
  121.1 42.9 all-gather.4
Sparse Core Ops, SparseCore 1:
  92.6 22.0 reduce-scatter.1
  118.2 33.4 all-reduce.2
where the time goes:
time: 177 us; the launch traced here: 176 us
  Pallas kernels  58.2 us (33%)
  blocking collectives  46.9 us (26%)
  waiting for transfers between devices  34.3 us (19%)
  between operations  15.6 us (9%)
  matrix products  12.1 us (7%)
  local copies, waits for them, and re-layouts  7.54 us (4%)
    pallas_call x1, Pallas kernels, fit_part(): pl.pallas_call(fit_kernel, grid=(aux // count,), in_specs=[pl.BlockSpec((...  30.3 us
    pallas_call x1, Pallas kernels, field_part(): pl.pallas_call(field_kernel, grid=(aux // count,), in_specs=[pl.BlockSpec...  27.9 us
    all_to_all x1, blocking collectives, body(): lax.all_to_all(amplitudes, 'occ', split_axis=2, concat_axis=1, tiled=True)  23.8 us
    psum x1, blocking collectives, body(): lax.psum(fit_part(amplitudes, fit_factor), 'occ').astype(jnp.bfloat16)  23.1 us
    reduce_scatter x1, waiting for transfers between devices, body(): lax.psum_scatter(part, 'aux', scatter_dimension=2, tiled=True)  19.7 us
    all_gather x1, waiting for transfers between devices, body(): lax.all_gather(field_cols, 'occ', axis=1, tiled=True).astype(jnp.float32)  10.5 us
    unnamed x12, local copies, waits for them, and re-layouts  4.83 us
  transfers between devices with their start and end apart: 4, of which 3 were waited for; matrix products, arithmetic and copies ran while one was open for 6% of the time, Pallas kernels for 33%

commit v1 on v0

v1 whole, which is shorter than its diff:
```python
import functools

import jax
import jax.numpy as jnp
from jax import lax
from jax.experimental import pallas as pl
from jax.experimental.pallas import tpu as pltpu
from jax.sharding import PartitionSpec as P

F32 = jnp.float32
BF16 = jnp.bfloat16
NT = (((1,), (1,)), ((), ()))
MESH = pl.DeviceIdType.MESH
STAGES = 4
CHUNK = 16
BATCH = 64
RESIDENT_BYTES = 52 << 20


def split3(value):
    hi = value.astype(BF16)
    rest = value - hi.astype(F32)
    mid = rest.astype(BF16)
    return hi, mid, (rest - mid.astype(F32)).astype(BF16)


def field_kernel(
    loose, x_ref, b_ref, out_ref,
    held, spare, xs_ref, sums, spread, sel, parts, acc, own, sent, got,
    load_sem, spare_sem, fit_send, fit_recv, part_send, part_recv,
):
    states, rows, virt = x_ref.shape
    aux = b_ref.shape[0]
    n_occ, n_aux = lax.axis_size("occ"), lax.axis_size("aux")
    occ_at, aux_at = lax.axis_index("occ"), lax.axis_index("aux")
    slab = virt // n_aux
    width = slab // STAGES
    kept = aux - loose
    kept_chunks, loose_chunks = kept // CHUNK, loose // CHUNK
    depth = CHUNK * rows
    wide = states * rows

    def load(c):
        at = pl.ds(c * CHUNK, CHUNK)
        return pltpu.make_async_copy(b_ref.at[at], held.at[at], load_sem.at[c])

    def spare_loads(k):
        return [
            pltpu.make_async_copy(
                b_ref.at[pl.ds(kept, loose), :, pl.ds(u * slab + k * width, width)],
                spare.at[k % 2, :, :, pl.ds(u * width, width)],
                spare_sem.at[k, u],
            )
            for u in range(n_aux)
        ]

    if loose:
        for k in (3, 2):
            for copy in spare_loads(k):
                copy.start()
    for c in range(kept_chunks):
        load(c).start()

    barrier = pltpu.get_barrier_semaphore()
    for d in range(1, n_occ):
        pl.semaphore_signal(
            barrier, inc=1, device_id=(lax.rem(occ_at + d, n_occ), aux_at), device_id_type=MESH
        )
    for d in range(1, n_aux):
        pl.semaphore_signal(
            barrier, inc=1, device_id=(occ_at, lax.rem(aux_at + d, n_aux)), device_id_type=MESH
        )

    if loose:
        for k in range(STAGES):
            for u in range(n_aux):
                at = u * slab + k * width
                xs_ref[k, :, :, u * width : (u + 1) * width] = x_ref[:, :, at : at + width]
    row = lax.broadcasted_iota(jnp.int32, sel.shape, 0)
    col = lax.broadcasted_iota(jnp.int32, sel.shape, 1)
    sel[...] = jnp.where(lax.rem(row, CHUNK) == col // rows, 1.0, 0.0).astype(BF16)

    groups = 2 if rows % 32 == 0 else 1
    part = rows // groups
    pick_row = lax.broadcasted_iota(jnp.int32, (CHUNK, CHUNK * part), 0)
    pick_col = lax.broadcasted_iota(jnp.int32, (CHUNK, CHUNK * part), 1)
    pick = jnp.where(pick_col // part == pick_row, 1.0, 0.0).astype(BF16)

    def fit_terms(block, left):
        terms = [None] * states
        lanes = block.shape[2]
        step = min(lanes, 256)
        for at in range(0, lanes, step):
            cols = slice(at, at + step)
            for s in range(states):
                total = None
                for g in range(groups):
                    line = slice(g * part, (g + 1) * part)
                    term = block[:, line, cols] * left[s : s + 1, line, cols]
                    total = term if total is None else total + term
                value = jnp.dot(
                    pick, total.reshape(CHUNK * part, step), preferred_element_type=F32
                )
                for half in range(0, step, 128):
                    piece = value[:, half : half + 128]
                    terms[s] = piece if terms[s] is None else terms[s] + piece
        return terms

    def loose_fit(k):
        for copy in spare_loads(k):
            copy.wait()

        def step(c, carry):
            terms = fit_terms(spare.at[k % 2, pl.ds(c * CHUNK, CHUNK)], xs_ref.at[k])
            at = pl.ds(kept + c * CHUNK, CHUNK)
            for s in range(states):
                if k == STAGES - 1:
                    sums[s, at, :] = terms[s]
                else:
                    sums[s, at, :] += terms[s]
            return carry

        lax.fori_loop(0, loose_chunks, step, 0)

    if loose:
        for k in (3, 2):
            loose_fit(k)
            for copy in spare_loads(k - 2):
                copy.start()

    def kept_fit(c, carry):
        load(c).wait()
        at = pl.ds(c * CHUNK, CHUNK)
        terms = fit_terms(held.at[at], x_ref)
        for s in range(states):
            sums[s, at, :] = terms[s]
        return carry

    lax.fori_loop(0, kept_chunks, kept_fit, 0)
    if loose:
        for k in (1, 0):
            loose_fit(k)

    ones = jnp.ones((8, 128), BF16)
    for s in range(states):
        fit = sum(
            lax.dot_general(ones, piece, NT, preferred_element_type=F32)
            for piece in split3(sums[s])
        )
        parts[occ_at, s : s + 1] = fit[:1]
    pl.semaphore_wait(barrier, n_occ + n_aux - 2)

    def fit_copy(d):
        return pltpu.make_async_remote_copy(
            src_ref=parts.at[occ_at],
            dst_ref=parts.at[occ_at],
            send_sem=fit_send.at[d],
            recv_sem=fit_recv.at[d],
            device_id=(lax.rem(occ_at + d, n_occ), aux_at),
            device_id_type=MESH,
        )

    for d in range(1, n_occ):
        fit_copy(d).start()
    for d in range(1, n_occ):
        fit_copy(d).wait()
    total = parts[0]
    for j in range(1, n_occ):
        total += parts[j]
    fitted = total.astype(BF16).astype(F32)
    n_chunks = aux // CHUNK
    at_row = lax.broadcasted_iota(jnp.int32, (n_chunks, aux), 0)
    at_col = lax.broadcasted_iota(jnp.int32, (n_chunks, aux), 1)
    mine = at_col // CHUNK == at_row
    for s in range(states):
        picked = jnp.where(mine, jnp.broadcast_to(fitted[s : s + 1], (n_chunks, aux)), 0.0)
        spread[s] = jnp.dot(picked.astype(BF16), sel[...], preferred_element_type=F32)

    lane = lax.broadcasted_iota(jnp.int32, (rows, depth), 1)
    line = lax.broadcasted_iota(jnp.int32, (rows, depth), 0)
    keep = lax.rem(lane, rows) == line

    def left_of(c):
        blocks = [
            jnp.concatenate(
                [
                    jnp.where(keep, jnp.broadcast_to(spread[s, pl.ds(q, 1)], (rows, depth)), 0.0)
                    for s in range(states)
                ],
                axis=0,
            ).astype(BF16)
            for q in [c * (BATCH // CHUNK) + n for n in range(BATCH // CHUNK)]
        ]
        return jnp.concatenate(blocks, axis=1)

    def part_copy(k, d):
        return pltpu.make_async_remote_copy(
            src_ref=sent.at[k, d],
            dst_ref=got.at[k, d],
            send_sem=part_send.at[k, d],
            recv_sem=part_recv.at[k, d],
            device_id=(occ_at, lax.rem(aux_at + d, n_aux)),
            device_id_type=MESH,
        )

    def piece_of(d):
        at = pl.multiple_of(lax.rem(aux_at + d, n_aux) * width, width)
        return acc[:, pl.ds(at, width)]

    def finish(k):
        for d in range(1, n_aux):
            part_copy(k, d).wait()
        value = own[k]
        for d in range(1, n_aux):
            value += got[k, d].astype(F32)
        out_ref[:, :, k * width : (k + 1) * width] = value.astype(BF16).reshape(states, rows, width)

    for k in range(STAGES):
        acc[...] = jnp.zeros_like(acc)
        if loose and k >= 2:
            for copy in spare_loads(k):
                copy.wait()

        def kept_step(c, carry):
            at = pl.ds(c * BATCH, BATCH)
            block = jnp.concatenate(
                [
                    held[at, :, u * slab + k * width : u * slab + (k + 1) * width].reshape(
                        BATCH * rows, width
                    )
                    for u in range(n_aux)
                ],
                axis=1,
            )
            acc[...] += jnp.dot(left_of(c), block, preferred_element_type=F32)
            return carry

        def loose_step(c, carry):
            block = spare[k % 2, pl.ds(c * BATCH, BATCH)].reshape(BATCH * rows, n_aux * width)
            acc[...] += jnp.dot(left_of(kept // BATCH + c), block, preferred_element_type=F32)
            return carry

        if loose:
            lax.fori_loop(0, loose // BATCH, loose_step, 0)
            if k < 2:
                for copy in spare_loads(k + 2):
                    copy.start()
        lax.fori_loop(0, kept // BATCH, kept_step, 0)
        own[k] = piece_of(0)
        for d in range(1, n_aux):
            sent[k, d] = piece_of(d).astype(BF16)
        for d in range(1, n_aux):
            part_copy(k, d).start()
        if k:
            finish(k - 1)
    finish(STAGES - 1)


def field_cols_of(amplitudes, factor):
    n_occ, n_aux = lax.axis_size("occ"), lax.axis_size("aux")
    states, rows, virt = amplitudes.shape
    aux = factor.shape[0]
    slab = virt // n_aux
    width = slab // STAGES
    wide = states * rows
    loose = aux // 4 if aux * rows * virt * 2 > RESIDENT_BYTES else 0
    dma = pltpu.SemaphoreType.DMA
    return pl.pallas_call(
        functools.partial(field_kernel, loose),
        out_shape=jax.ShapeDtypeStruct((states, rows, slab), BF16),
        in_specs=[pl.BlockSpec(memory_space=pltpu.VMEM), pl.BlockSpec(memory_space=pl.ANY)],
        out_specs=pl.BlockSpec(memory_space=pltpu.VMEM),
        scratch_shapes=[
            pltpu.VMEM((aux - loose, rows, virt), BF16),
            pltpu.VMEM((2, max(loose, 8), rows, n_aux * width), BF16),
            pltpu.VMEM((STAGES, states, rows, n_aux * width), BF16),
            pltpu.VMEM((states, aux, 128), F32),
            pltpu.VMEM((states, aux // CHUNK, CHUNK * rows), F32),
            pltpu.VMEM((aux, CHUNK * rows), BF16),
            pltpu.VMEM((n_occ, states, aux), F32),
            pltpu.VMEM((wide, n_aux * width), F32),
            pltpu.VMEM((STAGES, wide, width), F32),
            pltpu.VMEM((STAGES, n_aux, wide, width), BF16),
            pltpu.VMEM((STAGES, n_aux, wide, width), BF16),
            dma(((aux - loose) // CHUNK,)),
            dma((STAGES, n_aux)),
            dma((n_occ,)),
            dma((n_occ,)),
            dma((STAGES, n_aux)),
            dma((STAGES, n_aux)),
        ],
        compiler_params=pltpu.CompilerParams(
            collective_id=0, has_side_effects=True, vmem_limit_bytes=67_043_328
        ),
        cost_estimate=pl.CostEstimate(
            flops=4 * wide * aux * rows * virt,
            bytes_accessed=2 * aux * rows * virt,
            transcendentals=0,
        ),
    )(amplitudes, factor)


def body(amplitudes, fit_factor):
    high = lax.Precision.HIGHEST
    slab = lax.axis_index("aux")
    width = amplitudes.shape[2] // lax.axis_size("aux")
    own_cols = lax.dynamic_slice_in_dim(amplitudes, slab * width, width, 2)
    gathered = lax.all_gather(own_cols, "occ", axis=1, tiled=True)
    blocked = lax.all_to_all(amplitudes, "occ", split_axis=2, concat_axis=1, tiled=True)
    virtual_density = jnp.einsum(
        "sia,sib->sab", gathered, blocked, preferred_element_type=jnp.float32
    )
    pair_part = jnp.einsum("sia,sja->sij", own_cols, gathered, preferred_element_type=jnp.float32)
    occupied_density = lax.psum(pair_part, "aux")
    field_cols = field_cols_of(amplitudes, fit_factor)
    second = jnp.einsum(
        "sij,sja->sia",
        occupied_density,
        lax.all_gather(field_cols, "occ", axis=1, tiled=True).astype(jnp.float32),
        precision=high,
    )
    cross_part = jnp.einsum(
        "sib,sjb->sij", field_cols, gathered, preferred_element_type=jnp.float32
    )
    cross = lax.psum(cross_part, "aux")
    first = jnp.einsum("sij,sja->sia", cross, gathered.astype(jnp.float32), precision=high)
    return (virtual_density, occupied_density, first - second)


def solution(mesh):
    placed = (P(None, "occ", None), P("aux", "occ", None))
    return jax.shard_map(
        body,
        mesh=mesh,
        in_specs=placed,
        out_specs=(P(None, "aux", "occ"), P(None, "occ", None), P(None, "occ", "aux")),
        check_vma=False,
    )
```

time: 177 us -> 154 us (0.87)
  blocking collectives: 46.9 us -> 17.5 us
  waiting for transfers between devices: 34.3 us -> 46.5 us
  Pallas kernels: 58.2 us -> 55.3 us
  between operations: 15.6 us -> 13.8 us
    all_gather x1, waiting for transfers between devices: 10.5 us -> 40.7 us  [body(): lax.all_gather(field_cols, 'occ', axis=1, tiled=True).astype(jnp.float32)]
    psum x1 -> x0, blocking collectives: 23.1 us -> none  [body(): lax.psum(fit_part(amplitudes, fit_factor), 'occ').astype(jnp.bfloat16)]
    reduce_scatter x1 -> x0, waiting for transfers between devices: 19.7 us -> none  [body(): lax.psum_scatter(part, 'aux', scatter_dimension=2, tiled=True)]
    all_to_all x1, blocking collectives: 23.8 us -> 17.5 us  [body(): lax.all_to_all(amplitudes, 'occ', split_axis=2, concat_axis=1, tiled=True)]
    pallas_call x2 -> x1, Pallas kernels: 58.2 us -> 55.3 us  [field_cols_of(): pl.pallas_call(functools.partial(field_kernel, loose), out_shape=jax.Shap...]
    unnamed x12 -> x4, local copies, waits for them, and re-layouts: 4.83 us -> 5.38 us
  transfers between devices with their start and end apart: 4 -> 3, of which waited for: 3 -> 2; matrix products, arithmetic and copies ran while one was open for 6% -> 6% of each run, Pallas kernels for 33% -> 36%
where the time goes in v1:
time: 154 us; the launch traced here: 153 us
  Pallas kernels  55.3 us (36%)
  waiting for transfers between devices  46.5 us (30%)
  blocking collectives  17.5 us (11%)
  between operations  13.8 us (9%)
  matrix products  12.2 us (8%)
  local copies, waits for them, and re-layouts  7.69 us (5%)
    pallas_call x1, Pallas kernels, field_cols_of(): pl.pallas_call(functools.partial(field_kernel, loose), out_shape=jax.Shap...  55.3 us
    all_gather x1, waiting for transfers between devices, body(): lax.all_gather(field_cols, 'occ', axis=1, tiled=True).astype(jnp.float32)  40.7 us
    all_to_all x1, blocking collectives, body(): lax.all_to_all(amplitudes, 'occ', split_axis=2, concat_axis=1, tiled=True)  17.5 us
    unnamed x4, local copies, waits for them, and re-layouts  5.38 us
    psum x1, waiting for transfers between devices, body(): occupied_density = lax.psum(pair_part, 'aux')  5.15 us
  transfers between devices with their start and end apart: 3, of which 2 were waited for; matrix products, arithmetic and copies ran while one was open for 6% of the time, Pallas kernels for 36%

profile of v1, /device:TPU:0, one launch (start us, length us, event | category | flops | bytes accessed | tf_op | source)
XLA Modules:
  0.0 153.2 jit_solution(1587597639342943315)
XLA Ops:
  7.2 0.0 all-gather.3.cloned.1.call-start
  7.2 1.6 %constant_dynamic-slice_fusion = bf16[2,64,512]{2,1,0:T(8,128)(2,1)} fusion(bf16[2,64,2048]{2,1,0:T(8,128)(2,1)} %x_ref.1, s32[]{:T(128)S(6)} %select_n.3), kind=kLoop, calls=%fused_computation.1 | loop fusion | bytes 262148 | tf_op jit(solution)/shard_map/dynamic_slice | solution.py:307
  8.8 0.0 all-gather.3.cloned.1.call-update
  8.8 0.0 all-reduce.3.cloned.1.call-start
  8.9 55.3 %shard_map.49 = bf16[2,64,512]{2,1,0:T(8,128)(2,1)} custom-call(bf16[2,64,2048]{2,1,0:T(8,128)(2,1)} %x_ref.1, bf16[256,64,2048]{2,1,0:T(8,128)(2,1)} %b_ref.1), custom_call_target="tpu_custom_call" | custom-call | flops 17179869184 | bytes 67108864 | tf_op jit(solution)/shard_map/pallas_call | solution.py:268
  64.1 0.0 all-gather.3.cloned.1.call-done
  64.2 2.4 %fusion.1 = f32[2,64,512]{2,1,0:T(8,128)} fusion(bf16[2,64,512]{2,1,0:T(8,128)(2,1)} %constant_dynamic-slice_fusion, bf16[2,512,512]{2,1,0:T(8,128)(2,1)} %all-gather.3.cloned.1.call-done), kind=kOutput, calls=%fused_computation.3 | convolution fusion | flops 67108864 | bytes 1441792 | tf_op jit(solution)/shard_map/sia,sja->sij/dot_general | solution.py:313
  66.6 2.4 %fusion.2 = f32[2,64,512]{2,1,0:T(8,128)} fusion(bf16[2,64,512]{2,1,0:T(8,128)(2,1)} %shard_map.49, bf16[2,512,512]{2,1,0:T(8,128)(2,1)} %all-gather.3.cloned.1.call-done), kind=kOutput, calls=%fused_computation.4 | convolution fusion | flops 67108864 | bytes 1441792 | tf_op jit(solution)/shard_map/sib,sjb->sij/dot_general | solution.py:322
  69.1 0.0 all-reduce.3.cloned.1.call-update
  69.1 0.0 all-gather.5.cloned.1.call-start
  69.1 0.7 all-gather.5.cloned.1.call-update
  69.8 2.4 %copy.6 = bf16[2,64,2048]{1,0,2:T(2,128)(2,1)S(1)} copy(bf16[2,64,2048]{2,1,0:T(8,128)(2,1)} %x_ref.1) | data formatting | bytes 1048576 | tf_op args[0]
  72.2 0.7 reshape.6
  72.9 17.5 %all_to_all.18 = bf16[8,2,16384]{2,1,0:T(2,128)(2,1)S(1)} all-to-all(bf16[8,2,16384]{2,1,0:T(2,128)(2,1)S(1)} %reshape.6), channel_id=1, replica_groups=mesh['occ'=8,'aux'=4] {'occ'}, dimensions={0} | all-to-all | bytes 1048576 | tf_op jit(solution)/shard_map/all_to_all | solution.py:309
  90.4 0.7 reshape.7
  91.1 0.7 copy.7
  91.8 2.7 %fusion = f32[2,512,256]{2,1,0:T(8,128)} fusion(bf16[2,512,512]{2,1,0:T(8,128)(2,1)} %all-gather.3.cloned.1.call-done, bf16[2,512,256]{2,1,0:T(8,128)(2,1)S(1)} %bitcast.18), kind=kOutput, calls=%fused_computation.2 | convolution fusion | flops 268435456 | bytes 2621440 | tf_op jit(solution)/shard_map/sia,sib->sab/dot_general | solution.py:310
  94.5 5.2 %all-reduce.3.cloned.1.call-done = (f32[2,64,512]{2,1,0:T(8,128)}, f32[2,64,512]{2,1,0:T(8,128)}) async-done(((f32[2,64,512]{2,1,0:T(8,128)}, f32[2,64,512]{2,1,0:T(8,128)}), (f32[2,64,512]{2,1,0:T(8,128)}, f32[2,64,512]{2,1,0:T(8,128)})) %all-reduce.3.cloned.1.call-update) | async-done | bytes 524304 | tf_op jit(solution)/shard_map/psum | solution.py:314
  99.7 2.0 %fusion.3 = f32[2,64,512]{2,1,0:T(8,128)S(1)} fusion(f32[2,64,512]{2,1,0:T(8,128)} %get-tuple-element.4, bf16[2,512,512]{2,1,0:T(8,128)(2,1)} %all-gather.3.cloned.1.call-done), kind=kOutput, calls=%fused_computation.5 | convolution fusion | flops 402653184 | bytes 1572864 | tf_op jit(solution)/shard_map/sij,sja->sia/dot_general | solution.py:326
  101.7 40.7 %all-gather.5.cloned.1.call-done = bf16[2,512,512]{2,1,0:T(8,128)(2,1)} async-done(((bf16[2,64,512]{2,1,0:T(8,128)(2,1)}), bf16[2,512,512]{2,1,0:T(8,128)(2,1)}) %all-gather.5.cloned.1.call-update) | async-done | bytes 1048592 | tf_op jit(solution)/shard_map/all_gather | solution.py:319
  142.3 2.7 %convolution_subtract_fusion = f32[2,64,512]{2,1,0:T(8,128)} fusion(f32[2,64,512]{2,1,0:T(8,128)S(1)} %fusion.3, f32[2,64,512]{2,1,0:T(8,128)} %get-tuple-element.6, bf16[2,512,512]{2,1,0:T(8,128)(2,1)} %all-gather.5.cloned.1.call-done), kind=kOutput, calls=%fused_computation | convolution fusion | flops 402718720 | bytes 1835008 | tf_op jit(solution)/shard_map/sij,sja->sia/dot_general | solution.py:316
  145.0 1.7 %copy.10 = f32[2,64,512]{2,1,0:T(8,128)} copy(f32[2,64,512]{2,1,0:T(8,128)} %get-tuple-element.6) | data formatting | bytes 524288
Async XLA Ops:
  7.2 57.0 %all-gather.3.cloned.1.call-start = ((), (), s32[]{:S(2)}) async-start(), calls=%async_computation.1 | async-start | bytes 1179648 | tf_op jit(solution)/shard_map/all_gather | solution.py:308
  8.8 90.9 %all-reduce.3.cloned.1.call-start = ((), (), s32[]{:S(2)}) async-start(), calls=%async_computation.3 | async-start | bytes 1048576 | tf_op jit(solution)/shard_map/psum | solution.py:314
  69.1 73.2 %all-gather.5.cloned.1.call-start = ((), (), s32[]{:S(2)}) async-start(), calls=%async_computation.2 | async-start | bytes 1179648 | tf_op jit(solution)/shard_map/all_gather | solution.py:319
Sparse Core Ops, SparseCore 0:
  10.7 43.4 all-gather.2
  69.2 30.4 all-reduce.2
  101.9 40.3 all-gather.4

commit v2 on v1

v2 whole, which is shorter than its diff:
```python
import functools

import jax
import jax.numpy as jnp
from jax import lax
from jax.experimental import pallas as pl
from jax.experimental.pallas import tpu as pltpu
from jax.sharding import PartitionSpec as P

F32 = jnp.float32
BF16 = jnp.bfloat16
NT = (((1,), (1,)), ((), ()))
TN = (((0,), (0,)), ((), ()))
MESH = pl.DeviceIdType.MESH
STAGES = 4
CHUNK = 16
FIT = 16
BATCH = 64
RESIDENT_BYTES = 52 << 20


def split3(value):
    hi = value.astype(BF16)
    rest = value - hi.astype(F32)
    mid = rest.astype(BF16)
    return hi, mid, (rest - mid.astype(F32)).astype(BF16)


def wide_dot(left, right):
    hi, mid, _ = split3(left)
    return jnp.dot(hi, right, preferred_element_type=F32) + jnp.dot(
        mid, right, preferred_element_type=F32
    )


def densities_kernel(
    loose, x_ref, b_ref, vd_ref, od_ref, rs_ref,
    held, spare, xv, sums, spread, sel, parts, acc, own, sent, got,
    xs, xb, fg, od_part, od_got, od, cross, cross_out, vd, rs,
    load_sem, spare_sem, local_sem, fit_send, fit_recv, part_send, part_recv,
    xa_send, xa_recv, xf_send, xf_recv, xb_send, xb_recv, fa_send, fa_recv, ff_send, ff_recv,
    or_send, or_recv, oa_send, oa_recv, cr_send, cr_recv,
):
    states, rows, virt = x_ref.shape
    aux = b_ref.shape[0]
    n_occ, n_aux = lax.axis_size("occ"), lax.axis_size("aux")
    me, aux_at = lax.axis_index("occ"), lax.axis_index("aux")
    minor = 2 if n_occ % 2 == 0 else 1
    major = n_occ // minor
    row_at, side = me // minor, lax.rem(me, minor)
    slab = virt // n_aux
    width = slab // STAGES
    band = virt // n_occ
    block_w = xb.shape[2]
    occ = xs.shape[1]
    piece_w = occ // n_aux
    kept = aux - loose
    kept_chunks = kept // FIT
    depth = CHUNK * rows
    wide = states * rows
    slab_at = pl.multiple_of(aux_at * slab, slab)

    def lines(o):
        return pl.ds(pl.multiple_of(o * rows, rows), rows)

    def occ_peer(d):
        return lax.rem(me + d, n_occ), aux_at

    def aux_peer(d):
        return me, lax.rem(aux_at + d, n_aux)

    def far(d):
        return lax.rem(row_at + d, major) * minor + side, aux_at

    def near():
        return row_at * minor + (minor - 1 - side), aux_at

    def from_far(d):
        return lax.rem(row_at + major - d, major) * minor + side

    def remote(src, dst, send, recv, to):
        return pltpu.make_async_remote_copy(
            src_ref=src, dst_ref=dst, send_sem=send, recv_sem=recv, device_id=to, device_id_type=MESH
        )

    def load(c):
        at = pl.ds(c * FIT, FIT)
        return pltpu.make_async_copy(b_ref.at[at], held.at[at], load_sem.at[c])

    def spare_loads(k):
        return [
            pltpu.make_async_copy(
                b_ref.at[pl.ds(kept, loose), :, pl.ds(u * slab + k * width, width)],
                spare.at[k % 2, :, :, pl.ds(u * width, width)],
                spare_sem.at[k, u],
            )
            for u in range(n_aux)
        ]

    x_load = pltpu.make_async_copy(x_ref, xv, local_sem.at[0])
    own_cols = x_ref.at[:, :, pl.ds(slab_at, slab)]
    own_load = pltpu.make_async_copy(own_cols, xs.at[:, lines(me)], local_sem.at[1])
    x_load.start()
    if loose:
        for copy in spare_loads(3):
            copy.start()
    own_load.start()
    if loose:
        for copy in spare_loads(2):
            copy.start()
    for c in range(kept_chunks):
        load(c).start()

    barrier = pltpu.get_barrier_semaphore()
    for d in range(1, n_occ):
        pl.semaphore_signal(barrier, inc=1, device_id=occ_peer(d), device_id_type=MESH)
    for d in range(1, n_aux):
        pl.semaphore_signal(barrier, inc=1, device_id=aux_peer(d), device_id_type=MESH)

    row = lax.broadcasted_iota(jnp.int32, (CHUNK, depth), 0)
    col = lax.broadcasted_iota(jnp.int32, (CHUNK, depth), 1)
    pattern = jnp.where(row == col // rows, 1.0, 0.0).astype(BF16)
    for n in range(aux // CHUNK):
        sel[n * CHUNK : (n + 1) * CHUNK] = pattern
    pl.semaphore_wait(barrier, n_occ + n_aux - 2)

    def x_far(d):
        return remote(own_cols, xs.at[:, lines(me)], xa_send.at[d], xa_recv.at[d], far(d))

    def x_far_got(d):
        at = xs.at[:, lines(from_far(d))]
        return remote(at, at, xa_send.at[d], xa_recv.at[d], far(d))

    def x_near(d):
        at = xs.at[:, lines(from_far(d))]
        return remote(at if d else own_cols, at, xf_send.at[d], xf_recv.at[d], near())

    for d in range(1, major):
        x_far(d).start()
    if minor > 1:
        x_near(0).start()

    def x_forward(d):
        x_far_got(d).wait_recv()
        if minor > 1:
            x_near(d).start()

    fit_line = lax.broadcasted_iota(jnp.int32, (rows, wide), 0)
    fit_lane = lax.broadcasted_iota(jnp.int32, (rows, wide), 1)
    same = (lax.rem(fit_lane, rows) == fit_line)[None]

    def pair_sums(block, left):
        pairs = lax.dot_general(
            block.reshape(FIT * rows, left.shape[1]), left, NT, preferred_element_type=F32
        )
        return jnp.sum(jnp.where(same, pairs.reshape(FIT, rows, wide), 0.0), axis=1)

    def loose_fit(k):
        for copy in spare_loads(k):
            copy.wait()
        starts = [u * slab + k * width for u in range(n_aux)]

        def step(c, carry):
            left = jnp.concatenate([xv[:, :, a : a + width] for a in starts], axis=2)
            term = pair_sums(
                spare[k % 2, pl.ds(c * FIT, FIT)], left.reshape(wide, n_aux * width)
            )
            at = pl.ds(kept + c * FIT, FIT)
            if k == STAGES - 1:
                sums[at, :] = term
            else:
                sums[at, :] += term
            return carry

        lax.fori_loop(0, loose // FIT, step, 0)

    x_load.wait()
    if loose:
        for k in (3, 2):
            loose_fit(k)
            for copy in spare_loads(k - 2):
                copy.start()

    def kept_fit(c, carry):
        load(c).wait()
        at = pl.ds(c * FIT, FIT)
        sums[at, :] = pair_sums(held[at], xv[...].reshape(wide, virt))
        return carry

    done = 0
    for d in range(1, major):
        upto = kept_chunks * d // major
        lax.fori_loop(done, upto, kept_fit, 0)
        done = upto
        x_forward(d)
    lax.fori_loop(done, kept_chunks, kept_fit, 0)
    if loose:
        for k in (1, 0):
            loose_fit(k)

    ind_row = lax.broadcasted_iota(jnp.int32, (8, wide), 0)
    ind_col = lax.broadcasted_iota(jnp.int32, (8, wide), 1)
    ind = jnp.where(ind_col // rows == ind_row, 1.0, 0.0).astype(BF16)
    fit = sum(
        lax.dot_general(ind, piece, NT, preferred_element_type=F32) for piece in split3(sums[...])
    )
    parts[me] = fit[:states]

    def fit_copy(d):
        at = parts.at[me]
        return remote(at, at, fit_send.at[d], fit_recv.at[d], occ_peer(d))

    for d in range(1, n_occ):
        fit_copy(d).start()

    own_load.wait()
    if minor > 1:
        for d in range(major):
            x_near(d).wait_recv()
    for s in range(states):
        od_part[s] = lax.dot_general(xs[s, lines(me)], xs[s], NT, preferred_element_type=F32)

    def od_cols(u):
        return pl.ds(pl.multiple_of(u * piece_w, piece_w), piece_w)

    def od_reduce(d):
        to = aux_peer(d)
        return remote(od_part.at[:, :, od_cols(to[1])], od_got.at[d], or_send.at[d], or_recv.at[d], to)

    def od_share(d):
        at = od.at[:, :, od_cols(aux_at)]
        return remote(at, at, oa_send.at[d], oa_recv.at[d], aux_peer(d))

    for d in range(1, n_aux):
        od_reduce(d).start()

    holder = me * band // slab
    band_at = lax.rem(me * band, slab) // block_w * block_w
    band_cols = pl.ds(pl.multiple_of(band_at, block_w), block_w)
    mate = aux_at + 1 - 2 * lax.rem(aux_at, 2)
    along = lax.rem(aux_at, 2) == lax.rem(holder, 2)
    is_holder = aux_at == holder

    def band_copy(d, to):
        return remote(xs.at[:, :, band_cols], xb, xb_send.at[d], xb_recv, (me, to))

    relay = remote(xb, xb, xb_send.at[0], xb_recv, (me, mate))

    @pl.when(is_holder)
    def _():
        band_copy(0, mate).start()
        for d in range(2, n_aux, 2):
            band_copy(d, lax.rem(aux_at + d, n_aux)).start()
        xb[...] = xs[:, :, band_cols]

    for d in range(1, n_occ):
        fit_copy(d).wait()
    total = parts[0]
    for j in range(1, n_occ):
        total += parts[j]
    fitted = total.astype(BF16).astype(F32)
    n_chunks = aux // CHUNK
    at_row = lax.broadcasted_iota(jnp.int32, (n_chunks, aux), 0)
    at_col = lax.broadcasted_iota(jnp.int32, (n_chunks, aux), 1)
    mine = at_col // CHUNK == at_row
    for s in range(states):
        picked = jnp.where(mine, jnp.broadcast_to(fitted[s : s + 1], (n_chunks, aux)), 0.0)
        spread[s] = jnp.dot(picked.astype(BF16), sel[...], preferred_element_type=F32)

    lane = lax.broadcasted_iota(jnp.int32, (rows, depth), 1)
    line_at = lax.broadcasted_iota(jnp.int32, (rows, depth), 0)
    keep = lax.rem(lane, rows) == line_at

    def left_of(c):
        blocks = [
            jnp.concatenate(
                [
                    jnp.where(keep, jnp.broadcast_to(spread[s, pl.ds(q, 1)], (rows, depth)), 0.0)
                    for s in range(states)
                ],
                axis=0,
            ).astype(BF16)
            for q in [c * (BATCH // CHUNK) + n for n in range(BATCH // CHUNK)]
        ]
        return jnp.concatenate(blocks, axis=1)

    def part_copy(k, d):
        return remote(
            sent.at[k % 2, d], got.at[k, d], part_send.at[k, d], part_recv.at[k, d], aux_peer(d)
        )

    def piece_of(d):
        at = pl.multiple_of(lax.rem(aux_at + d, n_aux) * width, width)
        return acc[:, pl.ds(at, width)]

    def f_at(o, k):
        return fg.at[:, lines(o), pl.ds(k * width, width)]

    def f_far(k, d):
        at = f_at(me, k)
        return remote(at, at, fa_send.at[k, d], fa_recv.at[k, d], far(d))

    def f_far_got(k, d):
        at = f_at(from_far(d), k)
        return remote(at, at, fa_send.at[k, d], fa_recv.at[k, d], far(d))

    def f_near(k, d):
        at = f_at(from_far(d), k)
        return remote(at, at, ff_send.at[k, d], ff_recv.at[k, d], near())

    def finish(k):
        for d in range(1, n_aux):
            part_copy(k, d).wait()
        value = own[k % 2]
        for d in range(1, n_aux):
            value += got[k, d].astype(F32)
        value = value.astype(BF16).reshape(states, rows, width)
        fg[:, lines(me), k * width : (k + 1) * width] = value
        for d in range(1, major):
            f_far(k, d).start()
        if minor > 1:
            f_near(k, 0).start()
        for s in range(states):
            term = lax.dot_general(
                value[s], xs[s, :, k * width : (k + 1) * width], NT, preferred_element_type=F32
            )
            if k:
                cross[s] += term
            else:
                cross[s] = term

    def forward(k):
        for d in range(1, major):
            f_far_got(k, d).wait_recv()
            if minor > 1:
                f_near(k, d).start()

    def share_od():
        for d in range(1, n_aux):
            od_reduce(d).wait()
        value = od_part[:, :, od_cols(aux_at)]
        for d in range(1, n_aux):
            value += od_got[d]
        od[:, :, od_cols(aux_at)] = value
        for d in range(1, n_aux):
            od_share(d).start()

    for k in range(STAGES):
        acc[...] = jnp.zeros_like(acc)
        if loose and k >= 2:
            for copy in spare_loads(k):
                copy.wait()

        def kept_step(c, carry):
            at = pl.ds(c * BATCH, BATCH)
            block = jnp.concatenate(
                [
                    held[at, :, u * slab + k * width : u * slab + (k + 1) * width].reshape(
                        BATCH * rows, width
                    )
                    for u in range(n_aux)
                ],
                axis=1,
            )
            acc[...] += jnp.dot(left_of(c), block, preferred_element_type=F32)
            return carry

        def loose_step(c, carry):
            block = spare[k % 2, pl.ds(c * BATCH, BATCH)].reshape(BATCH * rows, n_aux * width)
            acc[...] += jnp.dot(left_of(kept // BATCH + c), block, preferred_element_type=F32)
            return carry

        if loose:
            lax.fori_loop(0, loose // BATCH, loose_step, 0)
            if k < 2:
                for copy in spare_loads(k + 2):
                    copy.start()
        lax.fori_loop(0, kept // BATCH - 1, kept_step, 0)
        if k:
            finish(k - 1)
        lax.fori_loop(kept // BATCH - 1, kept // BATCH, kept_step, 0)
        own[k % 2] = piece_of(0)
        for d in range(1, n_aux):
            sent[k % 2, d] = piece_of(d).astype(BF16)
        for d in range(1, n_aux):
            part_copy(k, d).start()
        if k == 0:
            share_od()
        if k >= 2:
            forward(k - 2)

    @pl.when(jnp.logical_not(is_holder))
    def _():
        relay.wait_recv()

        @pl.when(along)
        def _():
            relay.start()

    forward(STAGES - 2)
    finish(STAGES - 1)

    def cross_got(d):
        return held.at[pl.ds(d * states, states), :, pl.ds(0, occ)]

    def cross_copy(d):
        return remote(cross_out, cross_got(d), cr_send.at[d], cr_recv.at[d], aux_peer(d))

    cross_out[...] = cross[...].astype(BF16)
    for d in range(1, n_aux):
        cross_copy(d).start()

    vd_out = []
    for s in range(states):

        def vd_step(n, carry, s=s):
            at = pl.ds(pl.multiple_of(n * 128, 128), 128)
            value = lax.dot_general(xs[s, :, at], xb[s], TN, preferred_element_type=F32)
            if block_w > band:
                off = lax.rem(me * band, block_w)
                picked = value[:, :band]
                for m in range(1, block_w // band):
                    picked = jnp.where(off == m * band, value[:, m * band : (m + 1) * band], picked)
                value = picked
            vd[s, at] = value
            return carry

        lax.fori_loop(0, slab // 128, vd_step, 0)
        vd_out.append(pltpu.make_async_copy(vd.at[s], vd_ref.at[s], local_sem.at[2 + s]))
        vd_out[-1].start()

    forward(STAGES - 1)
    for d in range(1, n_aux):
        od_share(d).wait()
    od_out = pltpu.make_async_copy(od, od_ref, local_sem.at[0])
    od_out.start()
    for d in range(1, n_aux):
        cross_copy(d).wait()
    for s in range(states):
        total = cross[s]
        for d in range(1, n_aux):
            total += held[d * states + s, :, :occ].astype(F32)
        rs[s] = wide_dot(total, xs[s])
    if minor > 1:
        for k in range(STAGES):
            for d in range(major):
                f_near(k, d).wait_recv()
    for s in range(states):
        rs[s] = rs[s] - wide_dot(od[s], fg[s])
    rs_out = pltpu.make_async_copy(rs, rs_ref, local_sem.at[1])
    rs_out.start()

    for d in range(1, major):
        x_far(d).wait_send()
        for k in range(STAGES):
            f_far(k, d).wait_send()
    if minor > 1:
        for d in range(major):
            x_near(d).wait_send()
            for k in range(STAGES):
                f_near(k, d).wait_send()

    @pl.when(is_holder)
    def _():
        band_copy(0, mate).wait_send()
        for d in range(2, n_aux, 2):
            band_copy(d, lax.rem(aux_at + d, n_aux)).wait_send()

    @pl.when(jnp.logical_and(jnp.logical_not(is_holder), along))
    def _():
        relay.wait_send()

    for copy in vd_out:
        copy.wait()
    od_out.wait()
    rs_out.wait()


def body(amplitudes, factor):
    n_occ, n_aux = lax.axis_size("occ"), lax.axis_size("aux")
    states, rows, virt = amplitudes.shape
    aux = factor.shape[0]
    occ = rows * n_occ
    slab = virt // n_aux
    width = slab // STAGES
    band = virt // n_occ
    block_w = max(band, 128)
    wide = states * rows
    loose = aux // 4 if aux * rows * virt * 2 > RESIDENT_BYTES else 0
    major = n_occ // (2 if n_occ % 2 == 0 else 1)
    dma = pltpu.SemaphoreType.DMA
    whole = pl.BlockSpec(memory_space=pl.ANY)
    return pl.pallas_call(
        functools.partial(densities_kernel, loose),
        out_shape=(
            jax.ShapeDtypeStruct((states, slab, band), F32),
            jax.ShapeDtypeStruct((states, rows, occ), F32),
            jax.ShapeDtypeStruct((states, rows, slab), F32),
        ),
        in_specs=[whole] * 2,
        out_specs=(whole,) * 3,
        scratch_shapes=[
            pltpu.VMEM((aux - loose, rows, virt), BF16),
            pltpu.VMEM((2, max(loose, 8), rows, n_aux * width), BF16),
            pltpu.VMEM((states, rows, virt), BF16),
            pltpu.VMEM((aux, wide), F32),
            pltpu.VMEM((states, aux // CHUNK, CHUNK * rows), F32),
            pltpu.VMEM((aux, CHUNK * rows), BF16),
            pltpu.VMEM((n_occ, states, aux), F32),
            pltpu.VMEM((wide, n_aux * width), F32),
            pltpu.VMEM((2, wide, width), F32),
            pltpu.VMEM((2, n_aux, wide, width), BF16),
            pltpu.VMEM((STAGES, n_aux, wide, width), BF16),
            pltpu.VMEM((states, occ, slab), BF16),
            pltpu.VMEM((states, occ, block_w), BF16),
            pltpu.VMEM((states, occ, slab), BF16),
            pltpu.VMEM((states, rows, occ), F32),
            pltpu.VMEM((n_aux, states, rows, occ // n_aux), F32),
            pltpu.VMEM((states, rows, occ), F32),
            pltpu.VMEM((states, rows, occ), F32),
            pltpu.VMEM((states, rows, occ), BF16),
            pltpu.VMEM((states, slab, band), F32),
            pltpu.VMEM((states, rows, slab), F32),
            dma(((aux - loose) // FIT,)),
            dma((STAGES, n_aux)),
            dma((2 + states,)),
            dma((n_occ,)),
            dma((n_occ,)),
            dma((STAGES, n_aux)),
            dma((STAGES, n_aux)),
            dma((major,)),
            dma((major,)),
            dma((major,)),
            dma((major,)),
            dma((n_aux,)),
            dma(()),
            dma((STAGES, major)),
            dma((STAGES, major)),
            dma((STAGES, major)),
            dma((STAGES, major)),
            dma((n_aux,)),
            dma((n_aux,)),
            dma((n_aux,)),
            dma((n_aux,)),
            dma((n_aux,)),
            dma((n_aux,)),
        ],
        compiler_params=pltpu.CompilerParams(
            collective_id=0, has_side_effects=True, vmem_limit_bytes=67_043_328
        ),
        cost_estimate=pl.CostEstimate(
            flops=4 * wide * aux * rows * virt,
            bytes_accessed=2 * aux * rows * virt,
            transcendentals=0,
        ),
    )(amplitudes, factor)


def solution(mesh):
    placed = (P(None, "occ", None), P("aux", "occ", None))
    return jax.shard_map(
        body,
        mesh=mesh,
        in_specs=placed,
        out_specs=(P(None, "aux", "occ"), P(None, "occ", None), P(None, "occ", "aux")),
        check_vma=False,
    )
```

time: 154 us -> 84.6 us (0.55)
  waiting for transfers between devices: 46.5 us -> 0 us
  Pallas kernels: 55.3 us -> 78.1 us
  blocking collectives: 17.5 us -> 0 us
  between operations: 13.8 us -> 0.64 us
  matrix products: 12.2 us -> 0 us
  local copies, waits for them, and re-layouts: 7.69 us -> 5.6 us
    all_gather x2 -> x0, waiting for transfers between devices: 40.7 us -> none  [the longest x1 40.7 us: body(): lax.all_gather(field_cols, 'occ', axis=1, tiled=True).astype(jnp.float32)]
    pallas_call x1, Pallas kernels: 55.3 us -> 78.1 us  [body(): pl.pallas_call(functools.partial(densities_kernel, loose), out_shape=(jax...]
    all_to_all x1 -> x0, blocking collectives: 17.5 us -> none  [body(): lax.all_to_all(amplitudes, 'occ', split_axis=2, concat_axis=1, tiled=True)]
    dot_general x5 -> x0, matrix products: 12.2 us -> none  [the longest x1 2.73 us: body(): jnp.einsum('sia,sib->sab', gathered, blocked, preferred_element_type=jnp....]
    psum x1 -> x0, waiting for transfers between devices: 5.15 us -> none  [body(): occupied_density = lax.psum(pair_part, 'aux')]
    dynamic_slice x1 -> x0, local copies, waits for them, and re-layouts: 1.57 us -> none  [body(): own_cols = lax.dynamic_slice_in_dim(amplitudes, slab * width, width, 2)]
    unnamed x4 -> x3, local copies, waits for them, and re-layouts: 5.38 us -> 5.6 us
  transfers between devices with their start and end apart: 3 -> 0, of which waited for: 2 -> 0; matrix products, arithmetic and copies ran while one was open for 6% -> 0% of each run, Pallas kernels for 36% -> 0%
where the time goes in v2:
time: 84.6 us; the launch traced here: 84.4 us
  Pallas kernels  78.1 us (92%)
  local copies, waits for them, and re-layouts  5.6 us (7%)
    pallas_call x1, Pallas kernels, body(): pl.pallas_call(functools.partial(densities_kernel, loose), out_shape=(jax...  78.1 us
    unnamed x3, local copies, waits for them, and re-layouts  5.6 us

profile of v2, /device:TPU:0, one launch (start us, length us, event | category | flops | bytes accessed | tf_op | source)
XLA Modules:
  0.0 84.4 jit_solution(15279125822978177567)
XLA Ops:
  0.6 78.1 %shard_map.49 = (f32[2,512,256]{2,1,0:T(8,128)}, f32[2,64,512]{2,1,0:T(8,128)}, f32[2,64,512]{2,1,0:T(8,128)}) custom-call(bf16[2,64,2048]{2,1,0:T(8,128)(2,1)} %x_ref.1, bf16[256,64,2048]{2,1,0:T(8,128)(2,1)} %b_ref.1), custom_call_target="tpu_custom_call" | custom-call | flops 17179869184 | bytes 67108864 | tf_op jit(solution)/shard_map/pallas_call | solution.py:493
  78.8 2.3 %copy.8 = f32[2,512,256]{2,1,0:T(8,128)} copy(f32[2,512,256]{2,1,0:T(8,128)} %get-tuple-element.6) | data formatting | bytes 2097152
  81.0 1.7 %copy.9 = f32[2,64,512]{2,1,0:T(8,128)} copy(f32[2,64,512]{2,1,0:T(8,128)} %get-tuple-element.7) | data formatting | bytes 524288
  82.7 1.7 %copy.10 = f32[2,64,512]{2,1,0:T(8,128)} copy(f32[2,64,512]{2,1,0:T(8,128)} %get-tuple-element.8) | data formatting | bytes 524288

commit v3 on v2

--- a/solution.py
+++ b/solution.py
@@ -15,6 +15,8 @@
 STAGES = 4
 CHUNK = 16
 FIT = 16
+LOOSE_FIT = 32
+AHEAD = 4
 BATCH = 64
 RESIDENT_BYTES = 52 << 20
 
@@ -85,14 +87,14 @@
 
     def load(c):
         at = pl.ds(c * FIT, FIT)
-        return pltpu.make_async_copy(b_ref.at[at], held.at[at], load_sem.at[c])
+        return pltpu.make_async_copy(b_ref.at[at], held.at[at], load_sem.at[c % AHEAD])
 
     def spare_loads(k):
         return [
             pltpu.make_async_copy(
                 b_ref.at[pl.ds(kept, loose), :, pl.ds(u * slab + k * width, width)],
                 spare.at[k % 2, :, :, pl.ds(u * width, width)],
-                spare_sem.at[k, u],
+                spare_sem.at[k % 2, u],
             )
             for u in range(n_aux)
         ]
@@ -101,15 +103,15 @@
     own_cols = x_ref.at[:, :, pl.ds(slab_at, slab)]
     own_load = pltpu.make_async_copy(own_cols, xs.at[:, lines(me)], local_sem.at[1])
     x_load.start()
-    if loose:
-        for copy in spare_loads(3):
-            copy.start()
+    ahead = min(AHEAD, kept_chunks)
+    lead = 2 if loose else 0
+    for c in range(lead or ahead):
+        load(c).start()
     own_load.start()
     if loose:
-        for copy in spare_loads(2):
-            copy.start()
-    for c in range(kept_chunks):
-        load(c).start()
+        for k in (3, 2):
+            for copy in spare_loads(k):
+                copy.start()
 
     barrier = pltpu.get_barrier_semaphore()
     for d in range(1, n_occ):
@@ -151,9 +153,9 @@
 
     def pair_sums(block, left):
         pairs = lax.dot_general(
-            block.reshape(FIT * rows, left.shape[1]), left, NT, preferred_element_type=F32
+            block.reshape(block.shape[0] * rows, left.shape[1]), left, NT, preferred_element_type=F32
         )
-        return jnp.sum(jnp.where(same, pairs.reshape(FIT, rows, wide), 0.0), axis=1)
+        return jnp.sum(jnp.where(same, pairs.reshape(block.shape[0], rows, wide), 0.0), axis=1)
 
     def loose_fit(k):
         for copy in spare_loads(k):
@@ -163,55 +165,94 @@
         def step(c, carry):
             left = jnp.concatenate([xv[:, :, a : a + width] for a in starts], axis=2)
             term = pair_sums(
-                spare[k % 2, pl.ds(c * FIT, FIT)], left.reshape(wide, n_aux * width)
+                spare[k % 2, pl.ds(c * LOOSE_FIT, LOOSE_FIT)], left.reshape(wide, n_aux * width)
             )
-            at = pl.ds(kept + c * FIT, FIT)
+            at = pl.ds(kept + c * LOOSE_FIT, LOOSE_FIT)
             if k == STAGES - 1:
                 sums[at, :] = term
             else:
                 sums[at, :] += term
             return carry
 
-        lax.fori_loop(0, loose // FIT, step, 0)
+        lax.fori_loop(0, loose // LOOSE_FIT, step, 0)
+
+    ind_row = lax.broadcasted_iota(jnp.int32, (8, wide), 0)
+    ind_col = lax.broadcasted_iota(jnp.int32, (8, wide), 1)
+    ind = jnp.where(ind_col // rows == ind_row, 1.0, 0.0).astype(BF16)
+    spans = [(0, kept), (kept, loose)]
+
+    def fit_copy(g, d):
+        at = parts.at[g, me]
+        return remote(at, at, fit_send.at[g, d], fit_recv.at[g, d], occ_peer(d))
+
+    def send_fit(g):
+        start, size = spans[g]
+        pieces = split3(sums[start : start + size])
+        fit = sum(lax.dot_general(ind, p, NT, preferred_element_type=F32) for p in pieces)
+        parts[g, me] = jnp.zeros((states, aux), F32)
+        parts[g, me, :, :size] = fit[:states]
+        for d in range(1, n_occ):
+            fit_copy(g, d).start()
+
+    def spread_fit(g):
+        start, size = spans[g]
+        for d in range(1, n_occ):
+            fit_copy(g, d).wait()
+        total = parts[g, 0, :, :size]
+        for j in range(1, n_occ):
+            total += parts[g, j, :, :size]
+        fitted = total.astype(BF16).astype(F32)
+        chunks = size // CHUNK
+        at_row = lax.broadcasted_iota(jnp.int32, (chunks, size), 0)
+        at_col = lax.broadcasted_iota(jnp.int32, (chunks, size), 1)
+        first = start // CHUNK
+        for s in range(states):
+            picked = jnp.where(
+                at_col // CHUNK == at_row, jnp.broadcast_to(fitted[s : s + 1], (chunks, size)), 0.0
+            )
+            spread[s, first : first + chunks] = jnp.dot(
+                picked.astype(BF16), sel[:size], preferred_element_type=F32
+            )
 
     x_load.wait()
+    def kept_sum(c):
+        at = pl.ds(c * FIT, FIT)
+        sums[at, :] = pair_sums(held[at], xv[...].reshape(wide, virt))
+
+    def kept_fit(c, carry):
+        load(c).wait()
+
+        @pl.when(c + ahead < kept_chunks)
+        def _():
+            load(c + ahead).start()
+
+        kept_sum(c)
+        return carry
+
+    def lead_fit(c, carry):
+        load(c).wait()
+        load(c + lead).start()
+        kept_sum(c)
+        return carry
+
     if loose:
+        lax.fori_loop(0, lead, lead_fit, 0)
         for k in (3, 2):
             loose_fit(k)
-            for copy in spare_loads(k - 2):
-                copy.start()
-
-    def kept_fit(c, carry):
-        load(c).wait()
-        at = pl.ds(c * FIT, FIT)
-        sums[at, :] = pair_sums(held[at], xv[...].reshape(wide, virt))
-        return carry
-
-    done = 0
+            load(2 * lead + 3 - k).start()
+
+    done = lead
     for d in range(1, major):
-        upto = kept_chunks * d // major
+        upto = lead + (kept_chunks - lead) * d // major
         lax.fori_loop(done, upto, kept_fit, 0)
         done = upto
         x_forward(d)
-    lax.fori_loop(done, kept_chunks, kept_fit, 0)
     if loose:
         for k in (1, 0):
-            loose_fit(k)
-
-    ind_row = lax.broadcasted_iota(jnp.int32, (8, wide), 0)
-    ind_col = lax.broadcasted_iota(jnp.int32, (8, wide), 1)
-    ind = jnp.where(ind_col // rows == ind_row, 1.0, 0.0).astype(BF16)
-    fit = sum(
-        lax.dot_general(ind, piece, NT, preferred_element_type=F32) for piece in split3(sums[...])
-    )
-    parts[me] = fit[:states]
-
-    def fit_copy(d):
-        at = parts.at[me]
-        return remote(at, at, fit_send.at[d], fit_recv.at[d], occ_peer(d))
-
-    for d in range(1, n_occ):
-        fit_copy(d).start()
+            for copy in spare_loads(k):
+                copy.start()
+    lax.fori_loop(done, kept_chunks, kept_fit, 0)
+    send_fit(0)
 
     own_load.wait()
     if minor > 1:
@@ -253,20 +294,14 @@
             band_copy(d, lax.rem(aux_at + d, n_aux)).start()
         xb[...] = xs[:, :, band_cols]
 
-    for d in range(1, n_occ):
-        fit_copy(d).wait()
-    total = parts[0]
-    for j in range(1, n_occ):
-        total += parts[j]
-    fitted = total.astype(BF16).astype(F32)
-    n_chunks = aux // CHUNK
-    at_row = lax.broadcasted_iota(jnp.int32, (n_chunks, aux), 0)
-    at_col = lax.broadcasted_iota(jnp.int32, (n_chunks, aux), 1)
-    mine = at_col // CHUNK == at_row
-    for s in range(states):
-        picked = jnp.where(mine, jnp.broadcast_to(fitted[s : s + 1], (n_chunks, aux)), 0.0)
-        spread[s] = jnp.dot(picked.astype(BF16), sel[...], preferred_element_type=F32)
-
+    if loose:
+        for k in (1, 0):
+            loose_fit(k)
+
+    if loose:
+        send_fit(1)
+
+    spread_fit(0)
     lane = lax.broadcasted_iota(jnp.int32, (rows, depth), 1)
     line_at = lax.broadcasted_iota(jnp.int32, (rows, depth), 0)
     keep = lax.rem(lane, rows) == line_at
@@ -370,21 +405,25 @@
             acc[...] += jnp.dot(left_of(kept // BATCH + c), block, preferred_element_type=F32)
             return carry
 
+        if k == 0:
+            lax.fori_loop(0, kept // BATCH, kept_step, 0)
+            if loose:
+                spread_fit(1)
         if loose:
             lax.fori_loop(0, loose // BATCH, loose_step, 0)
             if k < 2:
                 for copy in spare_loads(k + 2):
                     copy.start()
-        lax.fori_loop(0, kept // BATCH - 1, kept_step, 0)
+        if k:
+            lax.fori_loop(0, kept // BATCH, kept_step, 0)
+        own[k % 2] = piece_of(0)
+        for d in range(1, n_aux):
+            sent[k % 2, d] = piece_of(d).astype(BF16)
+        for d in range(1, n_aux):
+            part_copy(k, d).start()
         if k:
             finish(k - 1)
-        lax.fori_loop(kept // BATCH - 1, kept // BATCH, kept_step, 0)
-        own[k % 2] = piece_of(0)
-        for d in range(1, n_aux):
-            sent[k % 2, d] = piece_of(d).astype(BF16)
-        for d in range(1, n_aux):
-            part_copy(k, d).start()
-        if k == 0:
+        if k == 1:
             share_od()
         if k >= 2:
             forward(k - 2)
@@ -396,19 +435,6 @@
         @pl.when(along)
         def _():
             relay.start()
-
-    forward(STAGES - 2)
-    finish(STAGES - 1)
-
-    def cross_got(d):
-        return held.at[pl.ds(d * states, states), :, pl.ds(0, occ)]
-
-    def cross_copy(d):
-        return remote(cross_out, cross_got(d), cr_send.at[d], cr_recv.at[d], aux_peer(d))
-
-    cross_out[...] = cross[...].astype(BF16)
-    for d in range(1, n_aux):
-        cross_copy(d).start()
 
     vd_out = []
     for s in range(states):
@@ -429,6 +455,19 @@
         vd_out.append(pltpu.make_async_copy(vd.at[s], vd_ref.at[s], local_sem.at[2 + s]))
         vd_out[-1].start()
 
+    finish(STAGES - 1)
+
+    def cross_got(d):
+        return held.at[pl.ds(d * states, states), :, pl.ds(0, occ)]
+
+    def cross_copy(d):
+        return remote(cross_out, cross_got(d), cr_send.at[d], cr_recv.at[d], aux_peer(d))
+
+    cross_out[...] = cross[...].astype(BF16)
+    for d in range(1, n_aux):
+        cross_copy(d).start()
+
+    forward(STAGES - 2)
     forward(STAGES - 1)
     for d in range(1, n_aux):
         od_share(d).wait()
@@ -474,6 +513,42 @@
         copy.wait()
     od_out.wait()
     rs_out.wait()
+
+
+def results_kernel(*refs):
+    count = len(refs) // 3
+    given, results, held = refs[:count], refs[count : 2 * count], refs[2 * count : 3 * count]
+    sems = refs[3 * count]
+    spans = [(n, s) for n in range(count) for s in range(given[n].shape[0])]
+    ins, outs = [], []
+    for at, (n, s) in enumerate(spans):
+        ins.append(pltpu.make_async_copy(given[n].at[s], held[n].at[s], sems.at[at, 0]))
+        outs.append(pltpu.make_async_copy(held[n].at[s], results[n].at[s], sems.at[at, 1]))
+    for copy in ins:
+        copy.start()
+    for at in range(len(spans)):
+        ins[at].wait()
+        outs[at].start()
+    for copy in outs:
+        copy.wait()
+
+
+def write_results(*given):
+    whole = pl.BlockSpec(memory_space=pl.ANY)
+    count = len(given)
+    return pl.pallas_call(
+        results_kernel,
+        out_shape=tuple(jax.ShapeDtypeStruct(g.shape, g.dtype) for g in given),
+        in_specs=[whole] * count,
+        out_specs=(whole,) * count,
+        scratch_shapes=[
+            *[pltpu.VMEM(g.shape, g.dtype) for g in given],
+            pltpu.SemaphoreType.DMA((sum(g.shape[0] for g in given), 2)),
+        ],
+        cost_estimate=pl.CostEstimate(
+            flops=0, bytes_accessed=2 * sum(g.size * 4 for g in given), transcendentals=0
+        ),
+    )(*given)
 
 
 def body(amplitudes, factor):
@@ -490,7 +565,7 @@
     major = n_occ // (2 if n_occ % 2 == 0 else 1)
     dma = pltpu.SemaphoreType.DMA
     whole = pl.BlockSpec(memory_space=pl.ANY)
-    return pl.pallas_call(
+    densities = pl.pallas_call(
         functools.partial(densities_kernel, loose),
         out_shape=(
             jax.ShapeDtypeStruct((states, slab, band), F32),
@@ -506,7 +581,7 @@
             pltpu.VMEM((aux, wide), F32),
             pltpu.VMEM((states, aux // CHUNK, CHUNK * rows), F32),
             pltpu.VMEM((aux, CHUNK * rows), BF16),
-            pltpu.VMEM((n_occ, states, aux), F32),
+            pltpu.VMEM((2, n_occ, states, aux), F32),
             pltpu.VMEM((wide, n_aux * width), F32),
             pltpu.VMEM((2, wide, width), F32),
             pltpu.VMEM((2, n_aux, wide, width), BF16),
@@ -521,11 +596,11 @@
             pltpu.VMEM((states, rows, occ), BF16),
             pltpu.VMEM((states, slab, band), F32),
             pltpu.VMEM((states, rows, slab), F32),
-            dma(((aux - loose) // FIT,)),
-            dma((STAGES, n_aux)),
+            dma((AHEAD,)),
+            dma((2, n_aux)),
             dma((2 + states,)),
-            dma((n_occ,)),
-            dma((n_occ,)),
+            dma((2, n_occ)),
+            dma((2, n_occ)),
             dma((STAGES, n_aux)),
             dma((STAGES, n_aux)),
             dma((major,)),
@@ -554,6 +629,7 @@
             transcendentals=0,
         ),
     )(amplitudes, factor)
+    return write_results(*densities)
 
 
 def solution(mesh):

time: 84.6 us -> 64.5 us (0.76)
  Pallas kernels: 78.1 us -> 63.6 us
  local copies, waits for them, and re-layouts: 5.6 us -> 0 us
    pallas_call x1, Pallas kernels: 78.1 us -> 61.3 us  [body(): pl.pallas_call(functools.partial(densities_kernel, loose), out_shape=(jax...]
    unnamed x3 -> x0, local copies, waits for them, and re-layouts: 5.6 us -> none
    pallas_call x0 -> x1, Pallas kernels: none -> 2.28 us  [write_results(): pl.pallas_call(results_kernel, out_shape=tuple((jax.ShapeDtypeStruct(g.sh...]
where the time goes in v3:
time: 64.5 us; the launch traced here: 64.4 us
  Pallas kernels  63.6 us (99%)
  between operations  0.8 us (1%)
    pallas_call x1, Pallas kernels, body(): pl.pallas_call(functools.partial(densities_kernel, loose), out_shape=(jax...  61.3 us
    pallas_call x1, Pallas kernels, write_results(): pl.pallas_call(results_kernel, out_shape=tuple((jax.ShapeDtypeStruct(g.sh...  2.28 us

profile of v3, /device:TPU:0, one launch (start us, length us, event | category | flops | bytes accessed | tf_op | source)
XLA Modules:
  0.0 64.4 jit_solution(4480067372716206612)
XLA Ops:
  0.6 61.3 %shard_map.49 = (f32[2,512,256]{2,1,0:T(8,128)}, f32[2,64,512]{2,1,0:T(8,128)}, f32[2,64,512]{2,1,0:T(8,128)}) custom-call(bf16[2,64,2048]{2,1,0:T(8,128)(2,1)} %x_ref.1, bf16[256,64,2048]{2,1,0:T(8,128)(2,1)} %b_ref.1), custom_call_target="tpu_custom_call" | custom-call | flops 17179869184 | bytes 67108864 | tf_op jit(solution)/shard_map/pallas_call | solution.py:568
  61.9 2.3 %shard_map.50 = (f32[2,512,256]{2,1,0:T(8,128)}, f32[2,64,512]{2,1,0:T(8,128)}, f32[2,64,512]{2,1,0:T(8,128)}) custom-call(f32[2,512,256]{2,1,0:T(8,128)} %get-tuple-element.6.refs_0_, f32[2,64,512]{2,1,0:T(8,128)} %get-tuple-element.7.refs_1_, f32[2,64,512]{2,1,0:T(8,128)} %get-tuple-element.8.refs_2_), custom_call_target="tpu_custom_call" | custom-call | bytes 3145728 | tf_op jit(solution)/shard_map/pallas_call | solution.py:539

commit v4 on v3

--- a/solution.py
+++ b/solution.py
@@ -324,9 +324,9 @@
             sent.at[k % 2, d], got.at[k, d], part_send.at[k, d], part_recv.at[k, d], aux_peer(d)
         )
 
-    def piece_of(d):
+    def piece_of(k, d):
         at = pl.multiple_of(lax.rem(aux_at + d, n_aux) * width, width)
-        return acc[:, pl.ds(at, width)]
+        return acc[k % 2, :, pl.ds(at, width)]
 
     def f_at(o, k):
         return fg.at[:, lines(o), pl.ds(k * width, width)]
@@ -380,11 +380,8 @@
         for d in range(1, n_aux):
             od_share(d).start()
 
-    for k in range(STAGES):
-        acc[...] = jnp.zeros_like(acc)
-        if loose and k >= 2:
-            for copy in spare_loads(k):
-                copy.wait()
+    def kept_field(k):
+        acc[k % 2] = jnp.zeros(acc.shape[1:], F32)
 
         def kept_step(c, carry):
             at = pl.ds(c * BATCH, BATCH)
@@ -397,47 +394,73 @@
                 ],
                 axis=1,
             )
-            acc[...] += jnp.dot(left_of(c), block, preferred_element_type=F32)
+            acc[k % 2] += jnp.dot(left_of(c), block, preferred_element_type=F32)
             return carry
 
+        lax.fori_loop(0, kept // BATCH, kept_step, 0)
+
+    def loose_field(k):
         def loose_step(c, carry):
             block = spare[k % 2, pl.ds(c * BATCH, BATCH)].reshape(BATCH * rows, n_aux * width)
-            acc[...] += jnp.dot(left_of(kept // BATCH + c), block, preferred_element_type=F32)
+            acc[k % 2] += jnp.dot(left_of(kept // BATCH + c), block, preferred_element_type=F32)
             return carry
 
-        if k == 0:
-            lax.fori_loop(0, kept // BATCH, kept_step, 0)
-            if loose:
-                spread_fit(1)
+        lax.fori_loop(0, loose // BATCH, loose_step, 0)
+
+    kept_field(0)
+    kept_field(1)
+    if loose:
+        spread_fit(1)
+    for k in range(STAGES):
+        if k >= 2:
+            kept_field(k)
         if loose:
-            lax.fori_loop(0, loose // BATCH, loose_step, 0)
+            if k >= 2:
+                for copy in spare_loads(k):
+                    copy.wait()
+            loose_field(k)
             if k < 2:
                 for copy in spare_loads(k + 2):
                     copy.start()
-        if k:
-            lax.fori_loop(0, kept // BATCH, kept_step, 0)
-        own[k % 2] = piece_of(0)
-        for d in range(1, n_aux):
-            sent[k % 2, d] = piece_of(d).astype(BF16)
+        own[k % 2] = piece_of(k, 0)
+        for d in range(1, n_aux):
+            sent[k % 2, d] = piece_of(k, d).astype(BF16)
         for d in range(1, n_aux):
             part_copy(k, d).start()
         if k:
             finish(k - 1)
         if k == 1:
             share_od()
+        if k == 2:
+
+            @pl.when(jnp.logical_and(jnp.logical_not(is_holder), along))
+            def _():
+                relay.wait_recv()
+                relay.start()
+
         if k >= 2:
             forward(k - 2)
 
-    @pl.when(jnp.logical_not(is_holder))
+    finish(STAGES - 1)
+
+    def cross_got(d):
+        return held.at[pl.ds(d * states, states), :, pl.ds(0, occ)]
+
+    def cross_copy(d):
+        return remote(cross_out, cross_got(d), cr_send.at[d], cr_recv.at[d], aux_peer(d))
+
+    cross_out[...] = cross[...].astype(BF16)
+    for d in range(1, n_aux):
+        cross_copy(d).start()
+
+    @pl.when(jnp.logical_not(along))
     def _():
         relay.wait_recv()
 
-        @pl.when(along)
-        def _():
-            relay.start()
-
     vd_out = []
     for s in range(states):
+        if s == 1:
+            forward(STAGES - 2)
 
         def vd_step(n, carry, s=s):
             at = pl.ds(pl.multiple_of(n * 128, 128), 128)
@@ -455,19 +478,6 @@
         vd_out.append(pltpu.make_async_copy(vd.at[s], vd_ref.at[s], local_sem.at[2 + s]))
         vd_out[-1].start()
 
-    finish(STAGES - 1)
-
-    def cross_got(d):
-        return held.at[pl.ds(d * states, states), :, pl.ds(0, occ)]
-
-    def cross_copy(d):
-        return remote(cross_out, cross_got(d), cr_send.at[d], cr_recv.at[d], aux_peer(d))
-
-    cross_out[...] = cross[...].astype(BF16)
-    for d in range(1, n_aux):
-        cross_copy(d).start()
-
-    forward(STAGES - 2)
     forward(STAGES - 1)
     for d in range(1, n_aux):
         od_share(d).wait()
@@ -582,7 +592,7 @@
             pltpu.VMEM((states, aux // CHUNK, CHUNK * rows), F32),
             pltpu.VMEM((aux, CHUNK * rows), BF16),
             pltpu.VMEM((2, n_occ, states, aux), F32),
-            pltpu.VMEM((wide, n_aux * width), F32),
+            pltpu.VMEM((2, wide, n_aux * width), F32),
             pltpu.VMEM((2, wide, width), F32),
             pltpu.VMEM((2, n_aux, wide, width), BF16),
             pltpu.VMEM((STAGES, n_aux, wide, width), BF16),

time: 64.5 us -> 64.3 us (level)
  no operation moved by 1% of the time
where the time goes in v4:
time: 64.3 us; the launch traced here: 64 us
  Pallas kernels  63.2 us (98%)
  between operations  0.8 us (1%)
    pallas_call x1, Pallas kernels, body(): pl.pallas_call(functools.partial(densities_kernel, loose), out_shape=(jax...  60.9 us
    pallas_call x1, Pallas kernels, write_results(): pl.pallas_call(results_kernel, out_shape=tuple((jax.ShapeDtypeStruct(g.sh...  2.28 us

profile of v4, /device:TPU:0, one launch (start us, length us, event | category | flops | bytes accessed | tf_op | source)
XLA Modules:
  0.0 64.0 jit_solution(16734975830515764372)
XLA Ops:
  0.6 60.9 %shard_map.49 = (f32[2,512,256]{2,1,0:T(8,128)}, f32[2,64,512]{2,1,0:T(8,128)}, f32[2,64,512]{2,1,0:T(8,128)}) custom-call(bf16[2,64,2048]{2,1,0:T(8,128)(2,1)} %x_ref.1, bf16[256,64,2048]{2,1,0:T(8,128)(2,1)} %b_ref.1), custom_call_target="tpu_custom_call" | custom-call | flops 17179869184 | bytes 67108864 | tf_op jit(solution)/shard_map/pallas_call | solution.py:578
  61.6 2.3 %shard_map.50 = (f32[2,512,256]{2,1,0:T(8,128)}, f32[2,64,512]{2,1,0:T(8,128)}, f32[2,64,512]{2,1,0:T(8,128)}) custom-call(f32[2,512,256]{2,1,0:T(8,128)} %get-tuple-element.6.refs_0_, f32[2,64,512]{2,1,0:T(8,128)} %get-tuple-element.7.refs_1_, f32[2,64,512]{2,1,0:T(8,128)} %get-tuple-element.8.refs_2_), custom_call_target="tpu_custom_call" | custom-call | bytes 3145728 | tf_op jit(solution)/shard_map/pallas_call | solution.py:549
